TPU v7x, 256 devices: a whole 4x4x8 slice. The times are simulated.
256 devices in a mesh: panels: 256 (over z, x, y, core).
Axes of the slice: x: 4, y: 4, z: 8, core: 2. Of those that a mesh axis runs over, the one named last changes fastest.
Arguments:
- densities: bfloat16 [64, 524288], P(None, 'panels'), may hold values from -6 to 6
- cluster_basis: bfloat16 [64, 524288], P(None, 'panels'), may hold values from -0.125 to 0.125
- near_rows: int32 [49152], P('panels'), may hold values from 0 to 19, as said below
- near_blocks: bfloat16 [49152, 128, 128], P('panels'), may hold values from -0.15625 to 0.15625
- local_coef: bfloat16 [4096, 4, 64, 64], P('panels'), may hold values from -0.75 to 0.75
- level_coef: bfloat16 [256, 8, 64, 64], P('panels'), may hold values from -0.375 to 0.375
Outputs:
- adjoint_image: float32 [64, 524288], P(None, 'panels')
Inputs may be any that keep to these rules, and one draw needn't show every extreme that they name: For near-field block p with q = p mod 192, near_rows[p] - q // 12 lies in 0 to 4: a block reads leaf blocks at most 2 away in Morton order.
All inputs are finite; a program needn't handle non-finite values.
Results may differ from a plain program's by a relative error of at most 0.0024.
Values may be sent and summed in bfloat16 or wider, within the bound.
A program may use at most 64 MiB of HBM per device.

v0:
```python
import jax
import jax.numpy as jnp
from jax import lax
from jax.sharding import PartitionSpec as P

HB = 2


def padded(x, sides, width):
    for axis, dim in sides:
        count, length = (lax.axis_size(axis), x.shape[dim])
        up = [(i, (i + 1) % count) for i in range(count - 1)]
        down = [(j, i) for i, j in up]
        last = lax.slice_in_dim(x, length - width, length, axis=dim)
        first = lax.slice_in_dim(x, 0, width, axis=dim)
        before = lax.ppermute(last, axis, up)
        after = lax.ppermute(first, axis, down)
        x = jnp.concatenate([before, x, after], axis=dim)
    return x


def local(densities, cluster_basis, near_rows, near_blocks, local_coef, level_coef):
    f32 = jnp.float32
    highest = lax.Precision.HIGHEST
    width_rhs, pan_count = densities.shape
    width_rank = cluster_basis.shape[0]
    block_size = near_blocks.shape[1]
    block_count = pan_count // block_size
    pair_count = near_rows.shape[0]
    per_column = pair_count // block_count
    local_levels = block_count.bit_length() - 1
    extended = padded(densities, (("panels", 1),), HB * block_size)
    basis_three = cluster_basis.reshape(width_rank, block_count, block_size)
    dens_three = densities.reshape(width_rhs, block_count, block_size)
    block_summ = jnp.einsum("kbp,rbp->bkr", basis_three, dens_three, preferred_element_type=f32)
    own_sum = jnp.sum(block_summ, axis=0)
    devices = lax.axis_size("panels")
    levels = devices.bit_length() - 1
    everyone = lax.all_gather(own_sum[None], "panels", axis=0, tiled=True)
    my_index = lax.axis_index("panels")
    device_ids = jnp.arange(devices, dtype=jnp.int32)
    member = jnp.stack(
        [
            (
                jnp.right_shift(device_ids, level_no)
                == jnp.bitwise_xor(jnp.right_shift(my_index, level_no), 1)
            ).astype(f32)
            for level_no in range(levels)
        ]
    )
    level_in = jnp.dot(member, everyone.reshape(devices, -1), precision=highest).reshape(
        levels, width_rank, width_rhs
    )
    global_part = jnp.einsum("lkq,lkr->qr", level_coef[0].astype(f32), level_in, precision=highest)
    local_list = []
    for depth_no in range(local_levels):
        cluster_sums = block_summ.reshape(
            block_count >> depth_no, 1 << depth_no, width_rank, width_rhs
        ).sum(1)
        sibling = cluster_sums.reshape(-1, 2, width_rank, width_rhs)[:, ::-1].reshape(
            block_count >> depth_no, width_rank, width_rhs
        )
        local_list.append(jnp.repeat(sibling, 1 << depth_no, axis=0))
    local_in = jnp.stack(local_list, axis=1)
    local_part = jnp.einsum("bjkq,bjkr->bqr", local_coef.astype(f32), local_in, precision=highest)
    coupled = (local_part + global_part[None]).astype(jnp.bfloat16)
    far = jnp.einsum("kbp,bkr->rbp", basis_three, coupled, preferred_element_type=f32)
    ext_blocks = extended.reshape(width_rhs, block_count + 2 * HB, block_size)
    picked = jnp.take(ext_blocks, near_rows, axis=1)
    terms = jnp.einsum("pij,rpi->rpj", near_blocks, picked, preferred_element_type=f32)
    near = terms.reshape(width_rhs, block_count, per_column, block_size).sum(2)
    return (near + far).reshape(width_rhs, pan_count)


def solution(mesh):
    return jax.shard_map(
        local,
        mesh=mesh,
        in_specs=(
            P(None, "panels"),
            P(None, "panels"),
            P("panels"),
            P("panels", None, None),
            P("panels", None, None, None),
            P("panels", None, None, None),
        ),
        out_specs=P(None, "panels"),
        check_vma=False,
    )
```

profile of v0, /device:TPU:1, one launch (start us, length us, event | category | flops | bytes accessed | tf_op | source)
XLA Modules:
  0.0 161.7 jit_solution(9124341210367585032)
XLA Ops:
  6.5 0.0 copy-start
  6.5 0.0 all-gather.3.cloned.1.call-start
  6.5 1.4 bitcast_reduce_fusion
  8.0 0.7 reduce_sum.53
  8.6 0.0 all-gather.3.cloned.1.call-update
  8.6 0.8 fusion.38
  9.4 4.6 %collective-permute-start = (bf16[64,256]{1,0:T(8,128)(2,1)S(1)}, bf16[64,256]{1,0:T(8,128)(2,1)S(1)}, u32[]{:S(2)}, u32[]{:S(2)}) collective-permute-start(bf16[64,256]{1,0:T(8,128)(2,1)S(1)} %get-tuple-element.5), channel_id=1, source_target_pairs={{0,1},{1,2},{2,3},{3,4},{4,5},{5,6},{6,7},{7,8},{8,9},{9,10},{10,1... | collective-permute-start | bytes 98312 | tf_op jit(solution)/shard_map/ppermute | solution.py:16
  14.0 1.9 %collective-permute-start.1 = (bf16[64,256]{1,0:T(8,128)(2,1)S(1)}, bf16[64,256]{1,0:T(8,128)(2,1)S(1)}, u32[]{:S(2)}, u32[]{:S(2)}) collective-permute-start(bf16[64,256]{1,0:T(8,128)(2,1)S(1)} %get-tuple-element.6), channel_id=1, source_target_pairs={{1,0},{2,1},{3,2},{4,3},{5,4},{6,5},{7,6},{8,7},{9,8},{10,9},{11,1... | collective-permute-start | bytes 98312 | tf_op jit(solution)/shard_map/ppermute | solution.py:17
  16.0 0.7 compare_select_fusion
  17.0 0.0 collective-permute-done
  17.0 2.3 %collective-permute-done.1 = bf16[64,256]{1,0:T(8,128)(2,1)S(1)} collective-permute-done((bf16[64,256]{1,0:T(8,128)(2,1)S(1)}, bf16[64,256]{1,0:T(8,128)(2,1)S(1)}, u32[]{:S(2)}, u32[]{:S(2)}) %collective-permute-start.1) | collective-permute-done | bytes 32800 | tf_op jit(solution)/shard_map/ppermute | solution.py:17
  19.3 0.1 copy_bitcast_fusion.1
  19.3 2.7 %gather_fusion = bf16[192,64,128]{2,1,0:T(8,128)(2,1)} fusion(bf16[64,20,128]{2,0,1:T(8,128)(2,1)S(1)} %copy_bitcast_fusion.1, s32[1024]{0:T(1024)S(1)} %pad_clamp_fusion), kind=kCustom, calls=%fused_computation | custom fusion | bytes 6292224 | tf_op jit(solution)/shard_map/jit(_take)/gather | solution.py:69
  22.0 8.3 %fusion = f32[192,64,128]{2,1,0:T(8,128)} fusion(bf16[192,128,128]{2,1,0:T(8,128)(2,1)} %param.9, bf16[192,64,128]{2,1,0:T(8,128)(2,1)} %gather_fusion, pred[192]{0:T(512)(128)(4,1)S(1)} %compare_and_fusion), kind=kOutput, calls=%fused_computation.1 | convolution fusion | flops 404226048 | bytes 15728832 | tf_op jit(solution)/shard_map/pij,rpi->rpj/dot_general | solution.py:70
  30.3 3.6 %reduce_sum.49 = f32[64,16,128]{2,0,1:T(8,128)S(1)} reduce(f32[64,16,12,128]{3,0,2,1:T(8,128)} %bitcast.82, f32[]{:T(128)} %constant.17.clone.1), dimensions={2}, to_apply=%region_0.0 | reduce | flops 1441792 | bytes 6815748 | tf_op jit(solution)/shard_map/reduce_sum | solution.py:71
  33.9 99.2 %all-gather.3.cloned.1.call-done = f32[16384,64]{1,0:T(8,128)} async-done(((f32[64,64]{1,0:T(8,128)}), f32[16384,64]{1,0:T(8,128)}) %all-gather.3.cloned.1.call-update) | async-done | bytes 4194320 | tf_op jit(solution)/shard_map/all_gather | solution.py:39
  133.1 7.9 %reshape.171 = f32[256,4096]{1,0:T(8,128)} reshape(f32[16384,64]{1,0:T(8,128)} %all-gather.3.cloned.1.call-done) | data formatting | bytes 8388608 | tf_op jit(solution)/shard_map/reshape | solution.py:51
  141.0 5.6 %copy.13 = f32[4096,256]{1,0:T(8,128)} copy(f32[4096,256]{0,1:T(8,128)} %bitcast.83) | data formatting | bytes 8388608 | tf_op jit(solution)/shard_map/dot_general | solution.py:51
  146.6 4.8 %fusion.34 = f32[8,64,64]{2,0,1:T(8,128)S(1)} fusion(f32[64,64,256]{2,1,0:T(8,128)} %bitcast.84, pred[8,256]{1,0:T(8,128)(4,1)S(1)} %stack.8), kind=kOutput, calls=%fused_computation.36 | convolution fusion | flops 100663296 | bytes 4327424 | tf_op jit(solution)/shard_map/dot_general | solution.py:51
  151.4 0.4 convolution_bitcast_fusion.1
  151.9 0.0 copy-start.2
  151.9 1.9 %fusion.21 = bf16[16,64,64]{1,2,0:T(8,128)(2,1)S(1)} fusion(f32[16,1,64,64]{3,2,0,1:T(8,128)S(1)} %bitcast.92, f32[16,1,64,64]{3,2,0,1:T(8,128)S(1)} %bitcast.88, f32[16,1,64,64]{3,2,0,1:T(8,128)S(1)} %bitcast.91, f32[16,1,64,64]{3,2,0,1:T(8,128)S(1)} %bitcast.93, bf16[16,4,64,64]{3,2,1,0:T(8,128)(2,1)S(1)} %copy-done, ...), kind=kOutput, calls=%fused_computation.19 | convolution fusion | flops 202244096 | bytes 1720320 | tf_op jit(solution)/shard_map/bjkq,bjkr->bqr/dot_general | solution.py:65
  153.8 0.2 fusion.14
  154.1 0.8 copy.44
  (24 shorter events, 0.4 us)
Async XLA Ops:
  6.5 145.4 %copy-start = (bf16[16,4,64,64]{3,2,1,0:T(8,128)(2,1)S(1)}, bf16[16,4,64,64]{3,2,1,0:T(8,128)(2,1)}, u32[]{:S(2)}) copy-start(bf16[16,4,64,64]{3,2,1,0:T(8,128)(2,1)} %param.10) | copy-start | bytes 1572868
  6.5 12.7 %copy-start.1 = (bf16[64,2048]{1,0:T(8,128)(2,1)S(1)}, bf16[64,2048]{1,0:T(8,128)(2,1)}, u32[]{:S(2)}) copy-start(bf16[64,2048]{1,0:T(8,128)(2,1)} %param.6) | copy-start | bytes 786436
  6.5 10.3 %copy-start.4 = (s32[192]{0:T(256)S(1)}, s32[192]{0:T(256)}, u32[]{:S(2)}) copy-start(s32[192]{0:T(256)} %param.8) | copy-start | bytes 2308
  6.5 126.6 %all-gather.3.cloned.1.call-start = ((), (), s32[]{:S(2)}) async-start(), calls=%async_computation | async-start | bytes 8421376 | tf_op jit(solution)/shard_map/all_gather | solution.py:39
  9.4 7.5 %collective-permute-start = (bf16[64,256]{1,0:T(8,128)(2,1)S(1)}, bf16[64,256]{1,0:T(8,128)(2,1)S(1)}, u32[]{:S(2)}, u32[]{:S(2)}) collective-permute-start(bf16[64,256]{1,0:T(8,128)(2,1)S(1)} %get-tuple-element.5), channel_id=1, source_target_pairs={{0,1},{1,2},{2,3},{3,4},{4,5},{5,6},{6,7},{7,8},{8,9},{9,10},{10,1... | collective-permute-start | bytes 98312 | tf_op jit(solution)/shard_map/ppermute | solution.py:16
  14.0 5.2 %collective-permute-start.1 = (bf16[64,256]{1,0:T(8,128)(2,1)S(1)}, bf16[64,256]{1,0:T(8,128)(2,1)S(1)}, u32[]{:S(2)}, u32[]{:S(2)}) collective-permute-start(bf16[64,256]{1,0:T(8,128)(2,1)S(1)} %get-tuple-element.6), channel_id=1, source_target_pairs={{1,0},{2,1},{3,2},{4,3},{5,4},{6,5},{7,6},{8,7},{9,8},{10,9},{11,1... | collective-permute-start | bytes 98312 | tf_op jit(solution)/shard_map/ppermute | solution.py:17
  146.6 4.8 %copy-start.3 = (bf16[1,8,64,64]{3,2,1,0:T(8,128)(2,1)S(1)}, bf16[1,8,64,64]{3,2,1,0:T(8,128)(2,1)}, u32[]{:S(2)}) copy-start(bf16[1,8,64,64]{3,2,1,0:T(8,128)(2,1)} %param.11) | copy-start | bytes 196612
  151.9 2.0 %copy-start.2 = (bf16[64,2048]{1,0:T(8,128)(2,1)S(1)}, bf16[64,2048]{1,0:T(8,128)(2,1)}, u32[]{:S(2)}) copy-start(bf16[64,2048]{1,0:T(8,128)(2,1)} %param.7) | copy-start | bytes 786436
Sparse Core Ops, SparseCore 0:
  11.1 122.0 all-gather.2
where the time goes:
time: 162 us
  waiting for transfers between devices  102 us (63%)
  local copies, waits for them, and re-layouts  18.1 us (11%)
  matrix products  16.9 us (10%)
  between operations  13.6 us (8%)
  starting transfers between devices  6.49 us (4%)
  other arithmetic  5.1 us (3%)
    all_gather x1, waiting for transfers between devices, local(): everyone = lax.all_gather(own_sum[None], 'panels', axis=0, tiled=True)  99.2 us
    dot_general x1, matrix products, local(): jnp.einsum('pij,rpi->rpj', near_blocks, picked, preferred_element_type=f32)  8.27 us
    reshape x1, local copies, waits for them, and re-layouts, local(): everyone.reshape(devices, -1)  7.89 us
    dot_general x1, local copies, waits for them, and re-layouts, local(): jnp.dot(member, everyone.reshape(devices, -1), precision=highest)  5.6 us
    dot_general x1, matrix products, local(): jnp.dot(member, everyone.reshape(devices, -1), precision=highest)  4.77 us
    ppermute x1, starting transfers between devices, padded(): before = lax.ppermute(last, axis, up)  4.57 us
    reduce_sum x1, other arithmetic, local(): near = terms.reshape(width_rhs, block_count, per_column, block_size).sum(2)  3.55 us
  transfers between devices with their start and end apart: 3, of which 2 were waited for; matrix products, arithmetic and copies ran while one was open for 10% of the time, Pallas kernels for 0%

commit v1 on v0

v1 whole, which is shorter than its diff:
```python
import functools

import jax
import jax.numpy as jnp
from jax import lax
from jax.experimental import pallas as pl
from jax.experimental.pallas import tpu as pltpu
from jax.sharding import PartitionSpec as P

HB = 2
MESH = pl.DeviceIdType.MESH
F32 = jnp.float32
BF16 = jnp.bfloat16
STAGES = ((0, 3), (3, 2), (5, 3))


def flipped(me, mask):
    out = me
    bit = 1
    while bit <= mask:
        if mask & bit:
            out = out + bit * (1 - 2 * ((me // bit) % 2))
        bit *= 2
    return out


def nt(a, b):
    return lax.dot_general(a, b, (((1,), (1,)), ((), ())), preferred_element_type=F32)


def split(x):
    hi = x.astype(BF16)
    lo = (x - hi.astype(F32)).astype(BF16)
    return hi, lo


def kernel(
    devices,
    dens_h,
    basis_h,
    rows_h,
    near_h,
    local_h,
    level_h,
    out_h,
    dens,
    basis,
    rows,
    near,
    local,
    level,
    left,
    right,
    acc,
    twin,
    part,
    sums,
    slots,
    levels,
    in_sem,
    dens_sem,
    near_sem,
    send_sem,
    recv_sem,
    halo_send,
    halo_recv,
    out_sem,
):
    me = lax.axis_index("panels")
    width = dens.shape[1]
    rank = basis.shape[0]
    leaves, depth, blk = near.shape
    per = depth // blk
    edge = left.shape[0] - HB

    peers = []
    for low, bits in STAGES:
        peers.append([flipped(me, k << low) for k in range(1, 1 << bits)])
    after = lax.rem(me + 1, devices)
    before = lax.rem(me + devices - 1, devices)

    barrier = pltpu.get_barrier_semaphore()
    everyone = [p for group in peers for p in group] + [after, before]
    for p in everyone:
        pl.semaphore_signal(barrier, inc=1, device_id=(p,), device_id_type=MESH)

    loads = [
        pltpu.make_async_copy(basis_h, basis, in_sem.at[0]),
        pltpu.make_async_copy(rows_h, rows, in_sem.at[1]),
        pltpu.make_async_copy(local_h, local, in_sem.at[2]),
        pltpu.make_async_copy(level_h, level, in_sem.at[3]),
    ]

    def dens_load(b, target, sem):
        return pltpu.make_async_copy(dens_h.at[:, pl.ds(b * blk, blk)], target, sem)

    dens_loads = [dens_load(b, dens.at[b], dens_sem.at[b]) for b in range(leaves)]
    edge_loads = [
        dens_load(b, left.at[HB + b], dens_sem.at[leaves + b]) for b in range(edge)
    ] + [
        dens_load(leaves - edge + b, right.at[b], dens_sem.at[leaves + edge + b]) for b in range(edge)
    ]
    near_loads = [
        pltpu.make_async_copy(near_h.at[c], near.at[c], near_sem.at[c]) for c in range(leaves)
    ]
    for copy in dens_loads + loads + edge_loads:
        copy.start()
    order = list(range(HB, leaves - HB)) + [0, 1, leaves - 2, leaves - 1]
    for c in order:
        near_loads[c].start()

    lane = lax.broadcasted_iota(jnp.int32, (width, 2 * rank), 1) < rank
    half = width // 2
    lane_half = lax.broadcasted_iota(jnp.int32, (half, 2 * rank), 1) < rank

    for copy in dens_loads:
        copy.wait()
    loads[0].wait()
    u_all = basis[...]
    x_all = jnp.concatenate([dens[b] for b in range(leaves)], axis=1)
    both = nt(x_all, jnp.concatenate([u_all, u_all], axis=0))
    sums[0] = jnp.where(lane_half, both[:half], both[half:])

    def sends(stage):
        first = sum((1 << bits) - 1 for _, bits in STAGES[:stage])
        return [
            pltpu.make_async_remote_copy(
                src_ref=sums.at[stage],
                dst_ref=slots.at[first + i],
                send_sem=send_sem.at[first + i],
                recv_sem=recv_sem.at[first + i],
                device_id=(p,),
                device_id_type=MESH,
            )
            for i, p in enumerate(peers[stage])
        ]

    pl.semaphore_wait(barrier, len(everyone))
    stage_copies = [sends(s) for s in range(len(STAGES))]

    for copy in stage_copies[0]:
        copy.start()
    halo = [
        pltpu.make_async_remote_copy(
            src_ref=dens.at[pl.ds(leaves - HB, HB)],
            dst_ref=left.at[pl.ds(0, HB)],
            send_sem=halo_send.at[0],
            recv_sem=halo_recv.at[0],
            device_id=(after,),
            device_id_type=MESH,
        ),
        pltpu.make_async_remote_copy(
            src_ref=dens.at[pl.ds(0, HB)],
            dst_ref=right.at[pl.ds(edge, HB)],
            send_sem=halo_send.at[1],
            recv_sem=halo_recv.at[1],
            device_id=(before,),
            device_id_type=MESH,
        ),
    ]
    for copy in halo:
        copy.start()

    def collect(stage):
        low, bits = STAGES[stage]
        first = sum((1 << b) - 1 for _, b in STAGES[:stage])
        total = sums[stage]
        for l in range(bits):
            value = None
            for k in range(1 << l, 2 << l):
                stage_copies[stage][k - 1].wait_recv()
                slot = slots[first + k - 1]
                value = slot if value is None else value + slot
            levels[low + l] = value
            total = total + value
        if stage + 1 < len(STAGES):
            sums[stage + 1] = total
            for copy in stage_copies[stage + 1]:
                copy.start()

    def near_leaf(c, source, shift):
        near_loads[c].wait()
        picked = []
        for i in range(per):
            at = jnp.clip(rows[c * per + i] - shift, 0, source.shape[0] - 1)
            picked.append(source[at])
        acc[:, c * blk : (c + 1) * blk] = jnp.dot(
            jnp.concatenate(picked, axis=1), near[c], preferred_element_type=F32
        )

    def local_part():
        loads[2].wait()
        tree = []
        leaf_sums = []
        for b in range(leaves):
            u = basis[:, b * blk : (b + 1) * blk]
            leaf_sums.append(nt(dens[b], jnp.concatenate([u, u], axis=0)))
        tree.append(leaf_sums)
        while len(tree[-1]) > 2:
            last = tree[-1]
            tree.append([last[2 * i] + last[2 * i + 1] for i in range(len(last) // 2)])
        for b in range(leaves):
            sib = [tree[j][(b >> j) ^ 1] for j in range(4)]
            value = jnp.concatenate(
                [jnp.where(lane, sib[0], sib[1]), jnp.where(lane, sib[2], sib[3])], axis=1
            )
            hi, lo = split(value)
            weight = local[b].reshape(4 * rank, rank)
            twice = jnp.dot(jnp.concatenate([hi, lo], axis=0), weight, preferred_element_type=F32)
            part[b] = twice[:width] + twice[width:]

    def global_part(l0, l1):
        values = jnp.concatenate([levels[l] for l in range(l0, l1)], axis=1)
        hi, lo = split(values)
        stacked = jnp.concatenate([hi, lo], axis=0)
        zero = jnp.zeros((rank, rank), BF16)
        tops, bottoms = [], []
        for l in range(l0, l1):
            tops += [level[l], zero]
            bottoms += [zero, level[l]]
        top = jnp.dot(stacked, jnp.concatenate(tops, axis=0), preferred_element_type=F32)
        bottom = jnp.dot(stacked, jnp.concatenate(bottoms, axis=0), preferred_element_type=F32)
        return jnp.concatenate([top[:half] + top[half:], bottom[:half] + bottom[half:]], axis=0)

    local_part()
    collect(0)
    loads[1].wait()
    for c in range(HB, HB + 5):
        near_leaf(c, dens, HB)
    collect(1)
    for c in range(HB + 5, leaves - HB):
        near_leaf(c, dens, HB)
    for copy in edge_loads:
        copy.wait()
    for copy in halo:
        copy.wait_recv()

    @pl.when(me == 0)
    def _():
        left[:HB] = jnp.zeros((HB, width, blk), BF16)

    @pl.when(me == devices - 1)
    def _():
        right[edge:] = jnp.zeros((HB, width, blk), BF16)

    for c in range(HB):
        near_leaf(c, left, 0)
    for c in range(leaves - HB, leaves):
        near_leaf(c, right, leaves - HB)
    loads[3].wait()
    twin[...] = global_part(0, 5)
    collect(2)

    glob = twin[...] + global_part(5, 8)
    outs = []
    for b in range(leaves):
        coupled = (part[b] + glob).astype(BF16)
        cols = slice(b * blk, (b + 1) * blk)
        acc[:, cols] = acc[:, cols] + jnp.dot(coupled, basis[:, cols], preferred_element_type=F32)
        if b % 4 == 3:
            chunk = pl.ds((b - 3) * blk, 4 * blk)
            copy = pltpu.make_async_copy(acc.at[:, chunk], out_h.at[:, chunk], out_sem.at[b // 4])
            copy.start()
            outs.append(copy)

    for group in stage_copies:
        for copy in group:
            copy.wait_send()
    for copy in halo:
        copy.wait_send()
    for copy in outs:
        copy.wait()


def local_step(devices, densities, cluster_basis, near_rows, near_blocks, local_coef, level_coef):
    width, pans = densities.shape
    rank = cluster_basis.shape[0]
    pairs, blk, _ = near_blocks.shape
    leaves = pans // blk
    per = pairs // leaves
    near = near_blocks.reshape(leaves, per * blk, blk)
    level = level_coef[0]
    n_slots = sum((1 << bits) - 1 for _, bits in STAGES)
    n_levels = level.shape[0]
    edge = 2 * HB
    any_space = pl.BlockSpec(memory_space=pl.ANY)
    return pl.pallas_call(
        functools.partial(kernel, devices),
        out_shape=jax.ShapeDtypeStruct((width, pans), F32),
        in_specs=[any_space] * 6,
        out_specs=any_space,
        scratch_shapes=[
            pltpu.VMEM((leaves, width, blk), BF16),
            pltpu.VMEM((rank, pans), BF16),
            pltpu.SMEM((pairs,), jnp.int32),
            pltpu.VMEM(near.shape, BF16),
            pltpu.VMEM(local_coef.shape, BF16),
            pltpu.VMEM(level.shape, BF16),
            pltpu.VMEM((edge + HB, width, blk), BF16),
            pltpu.VMEM((edge + HB, width, blk), BF16),
            pltpu.VMEM((width, pans), F32),
            pltpu.VMEM((width, rank), F32),
            pltpu.VMEM((leaves, width, rank), F32),
            pltpu.VMEM((len(STAGES), width // 2, 2 * rank), F32),
            pltpu.VMEM((n_slots, width // 2, 2 * rank), F32),
            pltpu.VMEM((n_levels, width // 2, 2 * rank), F32),
            pltpu.SemaphoreType.DMA((4,)),
            pltpu.SemaphoreType.DMA((leaves + 2 * edge,)),
            pltpu.SemaphoreType.DMA((leaves,)),
            pltpu.SemaphoreType.DMA((n_slots,)),
            pltpu.SemaphoreType.DMA((n_slots,)),
            pltpu.SemaphoreType.DMA((2,)),
            pltpu.SemaphoreType.DMA((2,)),
            pltpu.SemaphoreType.DMA((4,)),
        ],
        compiler_params=pltpu.CompilerParams(
            collective_id=0, has_side_effects=True, vmem_limit_bytes=56 * 1024 * 1024
        ),
        name="adjoint",
    )(densities, cluster_basis, near_rows, near, local_coef, level)


def solution(mesh):
    devices = mesh.shape["panels"]
    return jax.shard_map(
        functools.partial(local_step, devices),
        mesh=mesh,
        in_specs=(
            P(None, "panels"),
            P(None, "panels"),
            P("panels"),
            P("panels", None, None),
            P("panels", None, None, None),
            P("panels", None, None, None),
        ),
        out_specs=P(None, "panels"),
        check_vma=False,
    )
```

time: 162 us -> 26.5 us (0.16)
  the two profiles are of different devices: /device:TPU:1 before, /device:TPU:2 now
where the time goes in v1:
time: 26.5 us; the launch traced here: 26.4 us
  Pallas kernels  24.5 us (92%)
  local copies, waits for them, and re-layouts  1.87 us (7%)
    pallas_call x1, Pallas kernels, local_step(): pl.pallas_call(functools.partial(kernel, devices), out_shape=jax.ShapeDty...  24.5 us
    unnamed x1, local copies, waits for them, and re-layouts  1.87 us

profile of v1, /device:TPU:2, one launch (start us, length us, event | category | flops | bytes accessed | tf_op | source)
XLA Modules:
  0.0 26.4 jit_solution(17735984475356719022)
XLA Ops:
  0.0 24.5 %adjoint.1 = f32[64,2048]{1,0:T(8,128)} custom-call(bf16[64,2048]{1,0:T(8,128)(2,1)} %dens_h.1, bf16[64,2048]{1,0:T(8,128)(2,1)} %basis_h.1, s32[192]{0:T(256)} %rows_h.1, bf16[16,1536,128]{2,1,0:T(8,128)(2,1)} %bitcast.2, bf16[16,4,64,64]{3,2,1,0:T(8,128)(2,1)} %local_h.1, bf16[8,64,64]{2,1,0:T(8,128)(2,1)} %bitcast.3), custom_call_target="tpu_custom_call" | custom-call | tf_op jit(solution)/shard_map/adjoint/pallas_call | solution.py:287
  24.5 1.9 %copy.8 = f32[64,2048]{1,0:T(8,128)} copy(f32[64,2048]{1,0:T(8,128)} %adjoint.1) | data formatting | bytes 1048576
